TPU v7x, 128 devices: a whole 4x4x4 slice. The times are simulated.
128 devices in a mesh: grp: 4 (over y), dev: 32 (over z, x, core).
Axes of the slice: x: 4, y: 4, z: 4, core: 2. Of those that a mesh axis runs over, the one named last changes fastest.
Arguments:
- feeder_state: float32 [12288, 24, 256], P(('grp', 'dev')), may hold values from -6 to 6
- feeder_load: bfloat16 [12288, 24, 256], P(('grp', 'dev')), may hold values from -6 to 6
- feeder_inverse: bfloat16 [12288, 256, 256], P(('grp', 'dev')), as said below
- coupling: bfloat16 [12288, 256], P(('grp', 'dev')), may hold values from -0.375 to 0.375
- feeder_bus: int32 [12288], P(('grp', 'dev')), may hold values from 0 to 16383
- bus_coupling: bfloat16 [16384, 16384], P(('grp', 'dev')), may hold values from -0.09375 to 0.09375
- bus_diagonal: float32 [16384], P(('grp', 'dev')), may hold values from 1 to 3
- bus_load: float32 [24, 16384], P(None, ('grp', 'dev')), may hold values from -6 to 6
- bus_state: float32 [24, 16384], P(None, ('grp', 'dev')), may hold values from -6 to 6
- barrier: float32 [2], replicated, may hold values from 0.5 to 4
- step_length: float32 [2], replicated, may hold values from 0.4 to 1
Outputs:
- feeder_final: float32 [12288, 24, 256], P(('grp', 'dev'))
- bus_final: float32 [24, 16384], P(None, ('grp', 'dev'))
Inputs may be any that keep to these rules, and one draw needn't show every extreme that they name: `feeder_inverse`: each block is symmetric with a positive diagonal and is positive definite.
All inputs are finite; a program needn't handle non-finite values.
Results may differ from a plain program's by a relative error of at most 0.0022.
Values may be sent and summed in bfloat16 or wider, within the bound.
A program may use at most 128 MiB of HBM per device.

v0:
```python
import jax
import jax.numpy as jnp
from jax import lax
from jax.sharding import Mesh
from jax.sharding import PartitionSpec as P

GRP_DEV = ("grp", "dev_0", "dev_1", "dev_2")


def turned_gather(arrays, axis, dims):
    turned = [jnp.moveaxis(a, dim, 0) for a, dim in zip(arrays, dims)]
    widths = [t[0].size for t in turned]
    both = jnp.concatenate([t.reshape(-1, w) for t, w in zip(turned, widths)], axis=1)
    filled = lax.all_gather(both, axis, axis=0, tiled=True)
    blocks = jnp.split(filled, [sum(widths[:k]) for k in range(1, len(widths))], axis=1)
    return tuple(
        (
            jnp.moveaxis(b.reshape(-1, *t.shape[1:]), 0, dim)
            for b, t, dim in zip(blocks, turned, dims)
        )
    )


def from_everyone(array, axis):
    copies = jnp.broadcast_to(array, (lax.axis_size(axis), *array.shape))
    return lax.all_to_all(copies, axis, split_axis=0, concat_axis=0, tiled=True)


def joined_along(blocks, dim):
    blocks = jnp.moveaxis(blocks, 0, dim)
    lengths = blocks.shape
    return blocks.reshape(*lengths[:dim], lengths[dim] * lengths[dim + 1], *lengths[dim + 2 :])


def gather_axes(array, axes, dim):
    far, near = axes
    leading = from_everyone(array, far)
    blocks = jnp.swapaxes(from_everyone(leading, near), 0, 1)
    return joined_along(blocks.reshape(-1, *array.shape), dim)


def on_device(
    feeder_state,
    feeder_load,
    feeder_inverse,
    coupling,
    feeder_bus,
    bus_coupling,
    bus_diagonal,
    bus_load,
    bus_state,
    barrier,
    step_length,
):
    highest = lax.Precision.HIGHEST
    sensitivity = coupling.astype(jnp.float32)
    response = jnp.einsum(
        "fij,fj->fi", feeder_inverse, coupling, preferred_element_type=jnp.float32
    )
    schur = jnp.sum(sensitivity * response, axis=-1)
    bus_local = bus_coupling.shape[0]
    schur_all, buses_all = turned_gather((schur, feeder_bus.astype(jnp.float32)), GRP_DEV, (0, 0))
    bus_first = lax.axis_index(GRP_DEV) * bus_local
    owned = (
        buses_all.astype(jnp.int32)[:, None]
        == bus_first + jnp.arange(bus_local, dtype=jnp.int32)[None, :]
    ).astype(jnp.float32)
    bus_schur = jnp.dot(schur_all, owned, precision=highest)
    feeder_now = feeder_state
    bus_now = bus_state
    for iteration in range(barrier.shape[0]):
        weight_mu = barrier[iteration]
        residual = (
            feeder_load.astype(jnp.float32) + weight_mu * jax.nn.sigmoid(-feeder_now)
        ).astype(jnp.bfloat16)
        solved = jnp.einsum(
            "fij,fhj->fhi", feeder_inverse, residual, preferred_element_type=jnp.float32
        )
        boundary = jnp.sum(solved * sensitivity[:, None, :], axis=-1)
        boundary_all = gather_axes(boundary.T, (("grp", "dev_0", "dev_1"), "dev_2"), 1)
        bus_totals = jnp.dot(boundary_all, owned, precision=highest)
        bus_right = bus_load + weight_mu * jax.nn.sigmoid(-bus_now) - bus_totals
        pivots = bus_diagonal + weight_mu + bus_schur
        first_sweep = (bus_right / pivots).astype(jnp.bfloat16)
        coupled = jnp.einsum(
            "hk,bk->hb",
            gather_axes(first_sweep, (("grp", "dev_0", "dev_1"), "dev_2"), 1),
            bus_coupling,
            preferred_element_type=jnp.float32,
        )
        second_sweep = (bus_right - coupled) / pivots
        bus_now = bus_now + step_length[iteration] * second_sweep
        all_steps = gather_axes(second_sweep, (("grp", "dev_0", "dev_1"), "dev_2"), 1)
        at_feeder = jnp.take(all_steps, feeder_bus, axis=1)
        feeder_now = feeder_now + step_length[iteration] * (
            solved - response[:, None, :] * at_feeder.T[:, :, None]
        )
    return (feeder_now, bus_now)


def solution(mesh):
    split = Mesh(
        mesh.devices.reshape(mesh.shape["grp"], 4, 4, 2), ("grp", "dev_0", "dev_1", "dev_2")
    )
    in_specs = (
        P(GRP_DEV, None, None),
        P(GRP_DEV, None, None),
        P(GRP_DEV, None, None),
        P(GRP_DEV, None),
        P(GRP_DEV),
        P(GRP_DEV, None),
        P(GRP_DEV),
        P(None, GRP_DEV),
        P(None, GRP_DEV),
        P(),
        P(),
    )
    out_specs = (P(GRP_DEV, None, None), P(None, GRP_DEV))
    return jax.shard_map(
        on_device, mesh=split, in_specs=in_specs, out_specs=out_specs, check_vma=False
    )
```

profile of v0, /device:TPU:1, one launch (start us, length us, event | category | flops | bytes accessed | tf_op | source)
XLA Modules:
  0.0 255.7 jit_solution(10424992593101645294)
XLA Ops:
  0.6 1.3 fusion.43
  2.0 0.8 convert_element_type.29
  2.8 11.1 %multiply_reduce_fusion.1 = (f32[96,24]{1,0:T(8,128)S(1)}, f32[96,24,256]{2,1,0:T(8,128)}) fusion(f32[96,256]{1,0:T(8,128)S(1)} %convert_element_type.29, bf16[96,256,256]{2,1,0:T(8,128)(2,1)} %param.15, bf16[96,24,256]{2,1,0:T(8,128)(2,1)} %param.14, f32[96,24,256]{2,1,0:T(8,128)} %param.13, f32[]{:T(128)} %bitcast.1), kind=kOutput, calls=%fused_computation.21 | convolution fusion | flops 306706176 | bytes 18588676 | tf_op jit(solution)/shard_map/fij,fhj->fhi/dot_general | solution.py:76
  13.9 1.0 broadcast_in_dim.57
  14.9 12.0 %all-to-all-start = ((f32[64,24,96]{2,1,0:T(8,128)}), f32[64,24,96]{2,1,0:T(8,128)S(1)}, u32[]{:S(2)}, u32[]{:S(2)}) async-start(f32[64,24,96]{2,1,0:T(8,128)} %broadcast_in_dim.57), calls=%async_computation | async-start | bytes 1572864 | tf_op jit(solution)/shard_map/all_to_all | solution.py:26
  26.9 7.9 %fusion.37 = f32[96,1,256]{2,1,0:T(1,128)S(1)} fusion(bf16[96,256,256]{2,1,0:T(8,128)(2,1)} %param.15, bf16[96,256,1]{1,0,2:T(8,128)(2,1)S(1)} %bitcast.86), kind=kOutput, calls=%fused_computation.40 | convolution fusion | flops 12582912 | bytes 12730368 | tf_op jit(solution)/shard_map/fij,fj->fi/dot_general | solution.py:57
  34.8 0.1 multiply_reduce_fusion.2
  35.0 36.9 %all-gather = f32[128,96,2]{1,2,0:T(2,128)S(1)} all-gather(f32[1,96,2]{1,2,0:T(2,128)S(1)} %maximum_bitcast_fusion), channel_id=1, replica_groups=mesh['grp'=4,'dev_0'=4,'dev_1'=4,'dev_2'=2] {'grp','dev_0','dev_1','dev_2'}, dimensions={0}, use_global_device_ids=true | all-gather | bytes 99072 | tf_op jit(solution)/shard_map/all_gather | solution.py:14
  71.9 0.2 reshape.100
  72.2 3.9 %add_add_fusion = (f32[128]{0:T(128)S(1)}, f32[128]{0:T(128)S(1)}) fusion(f32[128]{0:T(128)S(1)} %copy-done.7, f32[]{:T(128)} %bitcast.24, f32[]{:T(128)} %bitcast.1, s32[128]{0:T(128)S(1)} %iota_add_fusion, s32[12288]{0:T(1024)S(1)} %bitcast.89, f32[12288,2]{0,1:T(2,128)S(1)} %reshape.100), kind=kOutput, calls=%fused_computation.55 | convolution fusion | flops 20447744 | bytes 100360 | tf_op jit(solution)/shard_map/dot_general | solution.py:68
  76.1 0.1 broadcast_in_dim.58
  76.2 4.8 %all_to_all.60 = f32[2,64,24,96]{3,2,1,0:T(8,128)S(1)} all-to-all(f32[2,64,24,96]{3,2,1,0:T(8,128)S(1)} %broadcast_in_dim.58), channel_id=1, replica_groups=mesh['grp'=4,'dev_0'=4,'dev_1'=4,'dev_2'=2] {'dev_2'}, dimensions={0} | all-to-all | bytes 2359296 | tf_op jit(solution)/shard_map/all_to_all | solution.py:26
  81.0 0.1 copy.36
  81.2 0.3 copy.37
  81.5 0.9 reshape.67
  82.4 3.3 %divide_convert_fusion.1 = (bf16[24,128]{1,0:T(8,128)(2,1)S(1)}, f32[24,128]{1,0:T(8,128)S(1)}) fusion(f32[128]{0:T(128)S(1)} %get-tuple-element.4, f32[24,12288]{1,0:T(8,128)S(1)} %reshape.67, s32[128]{0:T(128)S(1)} %iota_add_fusion, s32[12288]{0:T(1024)S(1)} %bitcast.90, f32[24,128]{1,0:T(8,128)S(1)} %copy-done.6, f32[24,128]{1,0:T(8,128)S(1)} %copy-done.3, ...), kind=kOutput, calls=%fused_computation.50 | convolution fusion | flops 454579200 | bytes 1272836 | tf_op jit(solution)/shard_map/dot_general | solution.py:81
  85.8 17.1 %all_to_all.61 = bf16[64,24,128]{2,1,0:T(8,128)(2,1)S(1)} all-to-all(bf16[64,24,128]{2,1,0:T(8,128)(2,1)S(1)} %broadcast_in_dim.59), channel_id=1, replica_groups=mesh['grp'=4,'dev_0'=4,'dev_1'=4,'dev_2'=2] {'grp','dev_0','dev_1'}, dimensions={0} | all-to-all | bytes 786432 | tf_op jit(solution)/shard_map/all_to_all | solution.py:26
  102.9 0.1 broadcast_in_dim.60
  103.0 6.1 %all_to_all.62 = bf16[2,64,24,128]{3,2,1,0:T(8,128)(2,1)S(1)} all-to-all(bf16[2,64,24,128]{3,2,1,0:T(8,128)(2,1)S(1)} %broadcast_in_dim.60), channel_id=1, replica_groups=mesh['grp'=4,'dev_0'=4,'dev_1'=4,'dev_2'=2] {'dev_2'}, dimensions={0} | all-to-all | bytes 1572864 | tf_op jit(solution)/shard_map/all_to_all | solution.py:26
  109.2 1.2 fusion.29
  110.4 1.0 broadcast_in_dim.61
  111.4 4.6 %all-to-all-start.4 = ((f32[64,24,128]{2,1,0:T(8,128)}), f32[64,24,128]{2,1,0:T(8,128)S(1)}, u32[]{:S(2)}, u32[]{:S(2)}) async-start(f32[64,24,128]{2,1,0:T(8,128)} %broadcast_in_dim.61), calls=%async_computation.4 | async-start | bytes 1572864 | tf_op jit(solution)/shard_map/all_to_all | solution.py:26
  116.1 0.6 fusion.42
  116.7 14.9 %all-to-all-done.4 = f32[64,24,128]{2,1,0:T(8,128)S(1)} async-done(((f32[64,24,128]{2,1,0:T(8,128)}), f32[64,24,128]{2,1,0:T(8,128)S(1)}, u32[]{:S(2)}, u32[]{:S(2)}) %all-to-all-start.4) | async-done | bytes 786464 | tf_op jit(solution)/shard_map/all_to_all | solution.py:26
  131.6 0.1 broadcast_in_dim.62
  131.7 6.2 %all_to_all.63 = f32[2,64,24,128]{3,2,1,0:T(8,128)S(1)} all-to-all(f32[2,64,24,128]{3,2,1,0:T(8,128)S(1)} %broadcast_in_dim.62), channel_id=1, replica_groups=mesh['grp'=4,'dev_0'=4,'dev_1'=4,'dev_2'=2] {'dev_2'}, dimensions={0} | all-to-all | bytes 3145728 | tf_op jit(solution)/shard_map/all_to_all | solution.py:26
  137.9 0.1 copy.41
  138.0 4.6 %copy.42 = f32[24,128,128]{0,2,1:T(8,128)} copy(f32[24,128,128]{2,0,1:T(8,128)S(1)} %bitcast.80) | data formatting | bytes 3145728 | tf_op jit(solution)/shard_map/transpose | solution.py:30
  142.7 4.0 %gather_fusion = f32[96,24]{1,0:T(8,128)S(1)} fusion(f32[24,16384]{0,1:T(8,128)} %bitcast.77, s32[1024]{0:T(1024)S(1)} %pad_clamp_fusion), kind=kCustom, calls=%fused_computation.clone | custom fusion | bytes 18816 | tf_op jit(solution)/shard_map/jit(_take)/gather | solution.py:94
  146.8 12.6 %multiply_reduce_fusion = (f32[96,24]{1,0:T(8,128)S(1)}, f32[96,24,256]{2,1,0:T(8,128)}) fusion(f32[96,256]{1,0:T(8,128)S(1)} %convert_element_type.29, bf16[96,256,256]{2,1,0:T(8,128)(2,1)} %param.15, bf16[96,24,256]{2,1,0:T(8,128)(2,1)S(1)} %copy-done.5, f32[]{:T(128)} %bitcast.24, f32[96,24,256]{2,1,0:T(8,128)} %param.13, ...), kind=kOutput, calls=%fused_computation.19 | convolution fusion | flops 309065472 | bytes 21055496 | tf_op jit(solution)/shard_map/fij,fhj->fhi/dot_general | solution.py:76
  159.5 19.3 %all_to_all.64 = f32[64,24,96]{2,1,0:T(8,128)S(1)} all-to-all(f32[64,24,96]{2,1,0:T(8,128)S(1)} %broadcast_in_dim.63), channel_id=1, replica_groups=mesh['grp'=4,'dev_0'=4,'dev_1'=4,'dev_2'=2] {'grp','dev_0','dev_1'}, dimensions={0} | all-to-all | bytes 1179648 | tf_op jit(solution)/shard_map/all_to_all | solution.py:26
  178.8 0.1 broadcast_in_dim.64
  178.9 6.5 %all_to_all.65 = f32[2,64,24,96]{3,2,1,0:T(8,128)S(1)} all-to-all(f32[2,64,24,96]{3,2,1,0:T(8,128)S(1)} %broadcast_in_dim.64), channel_id=1, replica_groups=mesh['grp'=4,'dev_0'=4,'dev_1'=4,'dev_2'=2] {'dev_2'}, dimensions={0} | all-to-all | bytes 2359296 | tf_op jit(solution)/shard_map/all_to_all | solution.py:26
  185.4 0.1 copy.44
  185.5 0.3 copy.45
  185.8 0.9 reshape.76
  186.8 3.8 %divide_convert_fusion = (bf16[24,128]{1,0:T(8,128)(2,1)S(1)}, f32[24,128]{1,0:T(8,128)S(1)}) fusion(f32[128]{0:T(128)S(1)} %get-tuple-element.3, f32[24,12288]{1,0:T(8,128)S(1)} %reshape.76, s32[128]{0:T(128)S(1)} %iota_add_fusion, s32[12288]{0:T(1024)S(1)} %bitcast.91, f32[24,128]{1,0:T(8,128)S(1)} %copy-done.6, f32[24,128]{1,0:T(8,128)S(1)} %copy-done.3, ...), kind=kOutput, calls=%fused_computation.48 | convolution fusion | flops 454585344 | bytes 1285128 | tf_op jit(solution)/shard_map/dot_general | solution.py:81
  190.6 15.2 %all_to_all.66 = bf16[64,24,128]{2,1,0:T(8,128)(2,1)S(1)} all-to-all(bf16[64,24,128]{2,1,0:T(8,128)(2,1)S(1)} %broadcast_in_dim.65), channel_id=1, replica_groups=mesh['grp'=4,'dev_0'=4,'dev_1'=4,'dev_2'=2] {'grp','dev_0','dev_1'}, dimensions={0} | all-to-all | bytes 786432 | tf_op jit(solution)/shard_map/all_to_all | solution.py:26
  205.8 0.1 broadcast_in_dim.66
  205.9 6.1 %all_to_all.67 = bf16[2,64,24,128]{3,2,1,0:T(8,128)(2,1)S(1)} all-to-all(bf16[2,64,24,128]{3,2,1,0:T(8,128)(2,1)S(1)} %broadcast_in_dim.66), channel_id=1, replica_groups=mesh['grp'=4,'dev_0'=4,'dev_1'=4,'dev_2'=2] {'dev_2'}, dimensions={0} | all-to-all | bytes 1572864 | tf_op jit(solution)/shard_map/all_to_all | solution.py:26
  212.1 2.9 %multiply_add_fusion.3 = (f32[24,128]{1,0:T(8,128)}, f32[24,128]{1,0:T(8,128)S(1)}) fusion(f32[]{:T(128)} %bitcast.23, f32[24,128]{1,0:T(8,128)S(1)} %copy-done.3, f32[24,128]{1,0:T(8,128)S(1)} %fusion.29, f32[]{:T(128)} %bitcast, f32[128]{0:T(128)S(1)} %get-tuple-element.3, f32[24,128]{1,0:T(8,128)S(1)} %get-tuple-element.18, ...), kind=kOutput, calls=%fused_computation.47 | convolution fusion | flops 100681728 | bytes 5042696 | tf_op jit(solution)/shard_map/hk,bk->hb/dot_general | solution.py:85
  215.1 19.5 %all_to_all.68 = f32[64,24,128]{2,1,0:T(8,128)S(1)} all-to-all(f32[64,24,128]{2,1,0:T(8,128)S(1)} %broadcast_in_dim.67), channel_id=1, replica_groups=mesh['grp'=4,'dev_0'=4,'dev_1'=4,'dev_2'=2] {'grp','dev_0','dev_1'}, dimensions={0} | all-to-all | bytes 1572864 | tf_op jit(solution)/shard_map/all_to_all | solution.py:26
  234.6 0.1 broadcast_in_dim.68
  234.7 6.5 %all_to_all.69 = f32[2,64,24,128]{3,2,1,0:T(8,128)S(1)} all-to-all(f32[2,64,24,128]{3,2,1,0:T(8,128)S(1)} %broadcast_in_dim.68), channel_id=1, replica_groups=mesh['grp'=4,'dev_0'=4,'dev_1'=4,'dev_2'=2] {'dev_2'}, dimensions={0} | all-to-all | bytes 3145728 | tf_op jit(solution)/shard_map/all_to_all | solution.py:26
  241.2 0.1 copy.48
  241.4 4.6 %copy.49 = f32[24,128,128]{0,2,1:T(8,128)} copy(f32[24,128,128]{2,0,1:T(8,128)S(1)} %bitcast.83) | data formatting | bytes 3145728 | tf_op jit(solution)/shard_map/transpose | solution.py:30
  246.0 4.0 %gather_fusion.1 = f32[96,24]{1,0:T(8,128)S(1)} fusion(f32[24,16384]{0,1:T(8,128)} %bitcast.76, s32[1024]{0:T(1024)S(1)} %pad_clamp_fusion), kind=kCustom, calls=%fused_computation.1.clone | custom fusion | bytes 18816 | tf_op jit(solution)/shard_map/jit(_take)/gather | solution.py:94
  250.1 5.6 %multiply_add_fusion = f32[96,24,256]{2,1,0:T(8,128)} fusion(f32[96,24,256]{2,1,0:T(8,128)} %get-tuple-element.16, f32[96,24]{1,0:T(8,128)S(1)} %broadcast_select_fusion, f32[]{:T(128)} %bitcast.23, f32[96,256]{1,0:T(8,128)S(1)} %bitcast.88, f32[96,24,256]{2,1,0:T(8,128)} %param.13, f32[96,24,256]{2,1,0:T(8,128)} %get-tuple-element.12, ...), kind=kLoop, calls=%fused_computation.18 | loop fusion | flops 4718592 | bytes 9553928 | tf_op jit(solution)/shard_map/add | solution.py:95
  (37 shorter events, 0.8 us)
Async XLA Ops:
  13.9 13.0 %copy-start.8 = (s32[96]{0:T(128)S(1)}, s32[96]{0:T(128)}, u32[]{:S(2)}) copy-start(s32[96]{0:T(128)} %param.17) | copy-start | bytes 1156
  13.9 13.0 %copy-start.2 = (bf16[96,256]{1,0:T(8,128)(2,1)S(1)}, bf16[96,256]{1,0:T(8,128)(2,1)}, u32[]{:S(2)}) copy-start(bf16[96,256]{1,0:T(8,128)(2,1)} %param.16) | copy-start | bytes 147460
  14.9 61.2 %all-to-all-start = ((f32[64,24,96]{2,1,0:T(8,128)}), f32[64,24,96]{2,1,0:T(8,128)S(1)}, u32[]{:S(2)}, u32[]{:S(2)}) async-start(f32[64,24,96]{2,1,0:T(8,128)} %broadcast_in_dim.57), calls=%async_computation | async-start | bytes 1572864 | tf_op jit(solution)/shard_map/all_to_all | solution.py:26
  26.9 45.3 %copy-start.7 = (f32[128]{0:T(128)S(1)}, f32[128]{0:T(128)}, u32[]{:S(2)}) copy-start(f32[128]{0:T(128)} %param.19) | copy-start | bytes 1540
  81.2 1.2 copy-start.3
  81.2 1.2 copy-start.6
  102.9 6.3 %copy-start = (bf16[128,16384]{1,0:T(8,128)(2,1)S(1)}, bf16[128,16384]{1,0:T(8,128)(2,1)}, u32[]{:S(2)}) copy-start(bf16[128,16384]{1,0:T(8,128)(2,1)} %param.18) | copy-start | bytes 12582916
  110.4 5.7 %copy-start.4 = (f32[2]{0:T(128)S(1)}, f32[2]{0:T(128)}, u32[]{:S(2)}) copy-start(f32[2]{0:T(128)} %param.23) | copy-start | bytes 28
  111.4 20.2 %all-to-all-start.4 = ((f32[64,24,128]{2,1,0:T(8,128)}), f32[64,24,128]{2,1,0:T(8,128)S(1)}, u32[]{:S(2)}, u32[]{:S(2)}) async-start(f32[64,24,128]{2,1,0:T(8,128)} %broadcast_in_dim.61), calls=%async_computation.4 | async-start | bytes 1572864 | tf_op jit(solution)/shard_map/all_to_all | solution.py:26
  138.0 8.7 %copy-start.5 = (bf16[96,24,256]{2,1,0:T(8,128)(2,1)S(1)}, bf16[96,24,256]{2,1,0:T(8,128)(2,1)}, u32[]{:S(2)}) copy-start(bf16[96,24,256]{2,1,0:T(8,128)(2,1)} %param.14) | copy-start | bytes 3538948
  205.8 6.3 %copy-start.1 = (bf16[128,16384]{1,0:T(8,128)(2,1)S(1)}, bf16[128,16384]{1,0:T(8,128)(2,1)}, u32[]{:S(2)}) copy-start(bf16[128,16384]{1,0:T(8,128)(2,1)} %param.18) | copy-start | bytes 12582916
where the time goes:
time: 257 us; the launch traced here: 256 us
  blocking collectives  144 us (56%)
  matrix products  46.7 us (18%)
  local copies, waits for them, and re-layouts  25.3 us (10%)
  starting transfers between devices  16.6 us (6%)
  waiting for transfers between devices  14.9 us (6%)
  other arithmetic  6.78 us (3%)
    all_to_all x10, blocking collectives, from_everyone(): return lax.all_to_all(copies, axis, split_axis=0, concat_axis=0, tiled=True)  107 us
    all_gather x1, blocking collectives, turned_gather(): filled = lax.all_gather(both, axis, axis=0, tiled=True)  36.9 us
    dot_general x2, matrix products, on_device(): jnp.einsum('fij,fhj->fhi', feeder_inverse, residual, preferred_element_ty...  23.7 us
    all_to_all x2, starting transfers between devices, from_everyone(): return lax.all_to_all(copies, axis, split_axis=0, concat_axis=0, tiled=True)  16.6 us
    all_to_all x2, waiting for transfers between devices, from_everyone(): return lax.all_to_all(copies, axis, split_axis=0, concat_axis=0, tiled=True)  14.9 us
    transpose x4, local copies, waits for them, and re-layouts, joined_along(): blocks = jnp.moveaxis(blocks, 0, dim)  9.86 us
    gather x2, local copies, waits for them, and re-layouts, on_device(): at_feeder = jnp.take(all_steps, feeder_bus, axis=1)  8 us
    dot_general x1, matrix products, on_device(): jnp.einsum('fij,fj->fi', feeder_inverse, coupling, preferred_element_type...  7.91 us
  transfers between devices with their start and end apart: 2, of which 1 were waited for; matrix products, arithmetic and copies ran while one was open for 5% of the time, Pallas kernels for 0%

commit v1 on v0

--- a/solution.py
+++ b/solution.py
@@ -11,7 +11,10 @@
     turned = [jnp.moveaxis(a, dim, 0) for a, dim in zip(arrays, dims)]
     widths = [t[0].size for t in turned]
     both = jnp.concatenate([t.reshape(-1, w) for t, w in zip(turned, widths)], axis=1)
-    filled = lax.all_gather(both, axis, axis=0, tiled=True)
+    devices = lax.axis_size(axis)
+    pieces = jnp.stack([both for _ in range(devices)])
+    pieces = lax.all_to_all(pieces, axis, split_axis=0, concat_axis=0)
+    filled = jnp.concatenate(pieces, axis=0)
     blocks = jnp.split(filled, [sum(widths[:k]) for k in range(1, len(widths))], axis=1)
     return tuple(
         (

time: 257 us -> 240 us (0.934)
  blocking collectives: 144 us -> 107 us
  waiting for transfers between devices: 14.9 us -> 25.9 us
  starting transfers between devices: 16.6 us -> 26.6 us
    all_gather x1 -> x0, blocking collectives: 36.9 us -> none  [turned_gather(): filled = lax.all_gather(both, axis, axis=0, tiled=True)]
    all_to_all x0 -> x1, starting transfers between devices: none -> 11.5 us  [turned_gather(): pieces = lax.all_to_all(pieces, axis, split_axis=0, concat_axis=0)]
    all_to_all x2, waiting for transfers between devices: 14.9 us -> 25.9 us  [from_everyone(): return lax.all_to_all(copies, axis, split_axis=0, concat_axis=0, tiled=True)]
  transfers between devices with their start and end apart: 2 -> 3, of which waited for: 1 -> 2; matrix products, arithmetic and copies ran while one was open for 5% -> 7% of each run, Pallas kernels for 0% -> 0%
where the time goes in v1:
time: 240 us
  blocking collectives  107 us (45%)
  matrix products  46.5 us (19%)
  starting transfers between devices  26.6 us (11%)
  waiting for transfers between devices  25.9 us (11%)
  local copies, waits for them, and re-layouts  25.4 us (11%)
  other arithmetic  6.83 us (3%)
    all_to_all x10, blocking collectives, from_everyone(): return lax.all_to_all(copies, axis, split_axis=0, concat_axis=0, tiled=True)  107 us
    all_to_all x2, waiting for transfers between devices, from_everyone(): return lax.all_to_all(copies, axis, split_axis=0, concat_axis=0, tiled=True)  25.9 us
    dot_general x2, matrix products, on_device(): jnp.einsum('fij,fhj->fhi', feeder_inverse, residual, preferred_element_ty...  23.1 us
    all_to_all x2, starting transfers between devices, from_everyone(): return lax.all_to_all(copies, axis, split_axis=0, concat_axis=0, tiled=True)  15.2 us
    all_to_all x1, starting transfers between devices, turned_gather(): pieces = lax.all_to_all(pieces, axis, split_axis=0, concat_axis=0)  11.5 us
    transpose x4, local copies, waits for them, and re-layouts, joined_along(): blocks = jnp.moveaxis(blocks, 0, dim)  9.89 us
    dot_general x1, matrix products, on_device(): jnp.einsum('fij,fj->fi', feeder_inverse, coupling, preferred_element_type...  8.06 us
    gather x2, local copies, waits for them, and re-layouts, on_device(): at_feeder = jnp.take(all_steps, feeder_bus, axis=1)  8 us
  transfers between devices with their start and end apart: 3, of which 2 were waited for; matrix products, arithmetic and copies ran while one was open for 7% of the time, Pallas kernels for 0%

profile of v1, /device:TPU:1, one launch (start us, length us, event | category | flops | bytes accessed | tf_op | source)
XLA Modules:
  0.0 239.6 jit_solution(10590095931794983814)
XLA Ops:
  0.6 0.7 compare_select_fusion
  1.4 8.1 %fusion.37 = f32[96,1,256]{2,1,0:T(1,128)S(1)} fusion(bf16[96,256,256]{2,1,0:T(8,128)(2,1)} %param.15, bf16[96,256,1]{1,0,2:T(8,128)(2,1)} %bitcast.84), kind=kOutput, calls=%fused_computation.40 | convolution fusion | flops 12582912 | bytes 12730368 | tf_op jit(solution)/shard_map/fij,fj->fi/dot_general | solution.py:60
  9.4 0.1 multiply_reduce_fusion.2
  9.6 0.7 stack.2
  10.3 11.5 %all-to-all-start.2 = ((f32[128,96,2]{1,2,0:T(2,128)}), f32[128,96,2]{1,2,0:T(2,128)S(1)}, u32[]{:S(2)}, u32[]{:S(2)}) async-start(f32[128,96,2]{1,2,0:T(2,128)} %stack.2), calls=%async_computation.2 | async-start | bytes 262144 | tf_op jit(solution)/shard_map/all_to_all | solution.py:16
  21.8 0.6 fusion.43
  22.5 10.4 %multiply_reduce_fusion.1 = (f32[96,24]{1,0:T(8,128)S(1)}, f32[96,24,256]{2,1,0:T(8,128)}) fusion(f32[96,256]{1,0:T(8,128)S(1)} %convert_element_type.29, bf16[96,256,256]{2,1,0:T(8,128)(2,1)} %param.15, bf16[96,24,256]{2,1,0:T(8,128)(2,1)} %param.14, f32[96,24,256]{2,1,0:T(8,128)S(1)} %copy-done.2, f32[]{:T(128)} %bitcast.1), kind=kOutput, calls=%fused_computation.21 | convolution fusion | flops 306706176 | bytes 18588676 | tf_op jit(solution)/shard_map/fij,fhj->fhi/dot_general | solution.py:79
  32.9 1.0 broadcast_in_dim.57
  33.9 10.5 %all-to-all-start = ((f32[64,24,96]{2,1,0:T(8,128)}), f32[64,24,96]{2,1,0:T(8,128)S(1)}, u32[]{:S(2)}, u32[]{:S(2)}) async-start(f32[64,24,96]{2,1,0:T(8,128)} %broadcast_in_dim.57), calls=%async_computation | async-start | bytes 1572864 | tf_op jit(solution)/shard_map/all_to_all | solution.py:29
  44.4 0.2 reshape.75
  44.7 3.9 %add_add_fusion = (f32[128]{0:T(128)S(1)}, f32[128]{0:T(128)S(1)}) fusion(f32[128]{0:T(128)S(1)} %copy-done.9, f32[]{:T(128)} %bitcast.23, f32[]{:T(128)} %bitcast.1, s32[128]{0:T(128)S(1)} %iota_add_fusion, s32[12288]{0:T(1024)S(1)} %bitcast.87, f32[12288,2]{0,1:T(2,128)S(1)} %reshape.75), kind=kOutput, calls=%fused_computation.55 | convolution fusion | flops 20447744 | bytes 100360 | tf_op jit(solution)/shard_map/dot_general | solution.py:71
  48.6 11.0 %all-to-all-done = f32[64,24,96]{2,1,0:T(8,128)S(1)} async-done(((f32[64,24,96]{2,1,0:T(8,128)}), f32[64,24,96]{2,1,0:T(8,128)S(1)}, u32[]{:S(2)}, u32[]{:S(2)}) %all-to-all-start) | async-done | bytes 589856 | tf_op jit(solution)/shard_map/all_to_all | solution.py:29
  59.7 0.1 broadcast_in_dim.58
  59.8 6.6 %all_to_all.65 = f32[2,64,24,96]{3,2,1,0:T(8,128)S(1)} all-to-all(f32[2,64,24,96]{3,2,1,0:T(8,128)S(1)} %broadcast_in_dim.58), channel_id=1, replica_groups=mesh['grp'=4,'dev_0'=4,'dev_1'=4,'dev_2'=2] {'dev_2'}, dimensions={0} | all-to-all | bytes 2359296 | tf_op jit(solution)/shard_map/all_to_all | solution.py:29
  66.3 0.1 copy.42
  66.5 0.3 copy.43
  66.8 0.9 reshape.72
  67.7 3.3 %divide_convert_fusion.1 = (bf16[24,128]{1,0:T(8,128)(2,1)S(1)}, f32[24,128]{1,0:T(8,128)S(1)}) fusion(f32[128]{0:T(128)S(1)} %get-tuple-element.4, f32[24,12288]{1,0:T(8,128)S(1)} %reshape.72, s32[128]{0:T(128)S(1)} %iota_add_fusion, s32[12288]{0:T(1024)S(1)} %bitcast.88, f32[24,128]{1,0:T(8,128)S(1)} %copy-done.8, f32[24,128]{1,0:T(8,128)S(1)} %copy-done.4, ...), kind=kOutput, calls=%fused_computation.50 | convolution fusion | flops 454579200 | bytes 1272836 | tf_op jit(solution)/shard_map/dot_general | solution.py:84
  71.1 15.2 %all_to_all.66 = bf16[64,24,128]{2,1,0:T(8,128)(2,1)S(1)} all-to-all(bf16[64,24,128]{2,1,0:T(8,128)(2,1)S(1)} %broadcast_in_dim.59), channel_id=1, replica_groups=mesh['grp'=4,'dev_0'=4,'dev_1'=4,'dev_2'=2] {'grp','dev_0','dev_1'}, dimensions={0} | all-to-all | bytes 786432 | tf_op jit(solution)/shard_map/all_to_all | solution.py:29
  86.3 0.1 broadcast_in_dim.60
  86.4 6.1 %all_to_all.67 = bf16[2,64,24,128]{3,2,1,0:T(8,128)(2,1)S(1)} all-to-all(bf16[2,64,24,128]{3,2,1,0:T(8,128)(2,1)S(1)} %broadcast_in_dim.60), channel_id=1, replica_groups=mesh['grp'=4,'dev_0'=4,'dev_1'=4,'dev_2'=2] {'dev_2'}, dimensions={0} | all-to-all | bytes 1572864 | tf_op jit(solution)/shard_map/all_to_all | solution.py:29
  92.6 1.2 fusion.29
  93.8 0.9 broadcast_in_dim.61
  94.8 4.6 %all-to-all-start.5 = ((f32[64,24,128]{2,1,0:T(8,128)}), f32[64,24,128]{2,1,0:T(8,128)S(1)}, u32[]{:S(2)}, u32[]{:S(2)}) async-start(f32[64,24,128]{2,1,0:T(8,128)} %broadcast_in_dim.61), calls=%async_computation.5 | async-start | bytes 1572864 | tf_op jit(solution)/shard_map/all_to_all | solution.py:29
  99.5 0.6 fusion.42
  100.1 14.9 %all-to-all-done.5 = f32[64,24,128]{2,1,0:T(8,128)S(1)} async-done(((f32[64,24,128]{2,1,0:T(8,128)}), f32[64,24,128]{2,1,0:T(8,128)S(1)}, u32[]{:S(2)}, u32[]{:S(2)}) %all-to-all-start.5) | async-done | bytes 786464 | tf_op jit(solution)/shard_map/all_to_all | solution.py:29
  115.1 6.2 %all_to_all.68 = f32[2,64,24,128]{3,2,1,0:T(8,128)S(1)} all-to-all(f32[2,64,24,128]{3,2,1,0:T(8,128)S(1)} %broadcast_in_dim.62), channel_id=1, replica_groups=mesh['grp'=4,'dev_0'=4,'dev_1'=4,'dev_2'=2] {'dev_2'}, dimensions={0} | all-to-all | bytes 3145728 | tf_op jit(solution)/shard_map/all_to_all | solution.py:29
  121.3 0.1 copy.47
  121.4 4.6 %copy.48 = f32[24,128,128]{0,2,1:T(8,128)} copy(f32[24,128,128]{2,0,1:T(8,128)S(1)} %bitcast.78) | data formatting | bytes 3145728 | tf_op jit(solution)/shard_map/transpose | solution.py:33
  126.1 4.0 %gather_fusion = f32[96,24]{1,0:T(8,128)S(1)} fusion(f32[24,16384]{0,1:T(8,128)} %bitcast.75, s32[1024]{0:T(1024)S(1)} %pad_clamp_fusion), kind=kCustom, calls=%fused_computation.clone | custom fusion | bytes 18816 | tf_op jit(solution)/shard_map/jit(_take)/gather | solution.py:97
  130.2 12.7 %multiply_reduce_fusion = (f32[96,24]{1,0:T(8,128)S(1)}, f32[96,24,256]{2,1,0:T(8,128)}) fusion(f32[96,256]{1,0:T(8,128)S(1)} %convert_element_type.29, bf16[96,256,256]{2,1,0:T(8,128)(2,1)} %param.15, bf16[96,24,256]{2,1,0:T(8,128)(2,1)S(1)} %copy-done.7, f32[]{:T(128)} %bitcast.23, f32[96,24,256]{2,1,0:T(8,128)} %param.13, ...), kind=kOutput, calls=%fused_computation.19 | convolution fusion | flops 309065472 | bytes 21055496 | tf_op jit(solution)/shard_map/fij,fhj->fhi/dot_general | solution.py:79
  143.0 19.3 %all_to_all.69 = f32[64,24,96]{2,1,0:T(8,128)S(1)} all-to-all(f32[64,24,96]{2,1,0:T(8,128)S(1)} %broadcast_in_dim.63), channel_id=1, replica_groups=mesh['grp'=4,'dev_0'=4,'dev_1'=4,'dev_2'=2] {'grp','dev_0','dev_1'}, dimensions={0} | all-to-all | bytes 1179648 | tf_op jit(solution)/shard_map/all_to_all | solution.py:29
  162.4 6.5 %all_to_all.70 = f32[2,64,24,96]{3,2,1,0:T(8,128)S(1)} all-to-all(f32[2,64,24,96]{3,2,1,0:T(8,128)S(1)} %broadcast_in_dim.64), channel_id=1, replica_groups=mesh['grp'=4,'dev_0'=4,'dev_1'=4,'dev_2'=2] {'dev_2'}, dimensions={0} | all-to-all | bytes 2359296 | tf_op jit(solution)/shard_map/all_to_all | solution.py:29
  168.9 0.1 copy.50
  169.0 0.3 copy.51
  169.4 0.9 reshape.82
  170.3 3.9 %divide_convert_fusion = (bf16[24,128]{1,0:T(8,128)(2,1)S(1)}, f32[24,128]{1,0:T(8,128)S(1)}) fusion(f32[128]{0:T(128)S(1)} %get-tuple-element.3, f32[24,12288]{1,0:T(8,128)S(1)} %reshape.82, s32[128]{0:T(128)S(1)} %iota_add_fusion, s32[12288]{0:T(1024)S(1)} %bitcast.89, f32[24,128]{1,0:T(8,128)S(1)} %copy-done.8, f32[24,128]{1,0:T(8,128)S(1)} %copy-done.4, ...), kind=kOutput, calls=%fused_computation.48 | convolution fusion | flops 454585344 | bytes 1285128 | tf_op jit(solution)/shard_map/dot_general | solution.py:84
  174.3 15.2 %all_to_all.71 = bf16[64,24,128]{2,1,0:T(8,128)(2,1)S(1)} all-to-all(bf16[64,24,128]{2,1,0:T(8,128)(2,1)S(1)} %broadcast_in_dim.65), channel_id=1, replica_groups=mesh['grp'=4,'dev_0'=4,'dev_1'=4,'dev_2'=2] {'grp','dev_0','dev_1'}, dimensions={0} | all-to-all | bytes 786432 | tf_op jit(solution)/shard_map/all_to_all | solution.py:29
  189.4 0.1 broadcast_in_dim.66
  189.5 6.1 %all_to_all.72 = bf16[2,64,24,128]{3,2,1,0:T(8,128)(2,1)S(1)} all-to-all(bf16[2,64,24,128]{3,2,1,0:T(8,128)(2,1)S(1)} %broadcast_in_dim.66), channel_id=1, replica_groups=mesh['grp'=4,'dev_0'=4,'dev_1'=4,'dev_2'=2] {'dev_2'}, dimensions={0} | all-to-all | bytes 1572864 | tf_op jit(solution)/shard_map/all_to_all | solution.py:29
  195.8 3.0 %multiply_add_fusion.3 = (f32[24,128]{1,0:T(8,128)}, f32[24,128]{1,0:T(8,128)S(1)}) fusion(f32[]{:T(128)} %bitcast.22, f32[24,128]{1,0:T(8,128)S(1)} %copy-done.4, f32[24,128]{1,0:T(8,128)S(1)} %fusion.29, f32[]{:T(128)} %bitcast, f32[128]{0:T(128)S(1)} %get-tuple-element.3, f32[24,128]{1,0:T(8,128)S(1)} %get-tuple-element.18, ...), kind=kOutput, calls=%fused_computation.47 | convolution fusion | flops 100681728 | bytes 5042696 | tf_op jit(solution)/shard_map/hk,bk->hb/dot_general | solution.py:88
  198.9 19.5 %all_to_all.73 = f32[64,24,128]{2,1,0:T(8,128)S(1)} all-to-all(f32[64,24,128]{2,1,0:T(8,128)S(1)} %broadcast_in_dim.67), channel_id=1, replica_groups=mesh['grp'=4,'dev_0'=4,'dev_1'=4,'dev_2'=2] {'grp','dev_0','dev_1'}, dimensions={0} | all-to-all | bytes 1572864 | tf_op jit(solution)/shard_map/all_to_all | solution.py:29
  218.4 0.1 broadcast_in_dim.68
  218.5 6.5 %all_to_all.74 = f32[2,64,24,128]{3,2,1,0:T(8,128)S(1)} all-to-all(f32[2,64,24,128]{3,2,1,0:T(8,128)S(1)} %broadcast_in_dim.68), channel_id=1, replica_groups=mesh['grp'=4,'dev_0'=4,'dev_1'=4,'dev_2'=2] {'dev_2'}, dimensions={0} | all-to-all | bytes 3145728 | tf_op jit(solution)/shard_map/all_to_all | solution.py:29
  225.0 0.1 copy.54
  225.1 4.6 %copy.55 = f32[24,128,128]{0,2,1:T(8,128)} copy(f32[24,128,128]{2,0,1:T(8,128)S(1)} %bitcast.81) | data formatting | bytes 3145728 | tf_op jit(solution)/shard_map/transpose | solution.py:33
  229.8 4.0 %gather_fusion.1 = f32[96,24]{1,0:T(8,128)S(1)} fusion(f32[24,16384]{0,1:T(8,128)} %bitcast.74, s32[1024]{0:T(1024)S(1)} %pad_clamp_fusion), kind=kCustom, calls=%fused_computation.1.clone | custom fusion | bytes 18816 | tf_op jit(solution)/shard_map/jit(_take)/gather | solution.py:97
  233.8 5.7 %multiply_add_fusion = f32[96,24,256]{2,1,0:T(8,128)} fusion(f32[96,24,256]{2,1,0:T(8,128)} %get-tuple-element.16, f32[96,24]{1,0:T(8,128)S(1)} %broadcast_select_fusion, f32[]{:T(128)} %bitcast.22, f32[96,256]{1,0:T(8,128)S(1)} %bitcast.86, f32[96,24,256]{2,1,0:T(8,128)} %param.13, f32[96,24,256]{2,1,0:T(8,128)} %get-tuple-element.12, ...), kind=kLoop, calls=%fused_computation.18 | loop fusion | flops 4718592 | bytes 9553928 | tf_op jit(solution)/shard_map/add | solution.py:98
  (43 shorter events, 1.0 us)
Async XLA Ops:
  1.4 8.1 %copy-start.3 = (bf16[96,256]{1,0:T(8,128)(2,1)S(1)}, bf16[96,256]{1,0:T(8,128)(2,1)}, u32[]{:S(2)}) copy-start(bf16[96,256]{1,0:T(8,128)(2,1)} %param.16) | copy-start | bytes 147460
  1.4 20.4 %copy-start.5 = (f32[2]{0:T(128)S(1)}, f32[2]{0:T(128)}, u32[]{:S(2)}) copy-start(f32[2]{0:T(128)} %param.22) | copy-start | bytes 28
  1.4 21.1 %copy-start.2 = (f32[96,24,256]{2,1,0:T(8,128)S(1)}, f32[96,24,256]{2,1,0:T(8,128)}, u32[]{:S(2)}) copy-start(f32[96,24,256]{2,1,0:T(8,128)} %param.13) | copy-start | bytes 7077892
  10.3 22.7 %all-to-all-start.2 = ((f32[128,96,2]{1,2,0:T(2,128)}), f32[128,96,2]{1,2,0:T(2,128)S(1)}, u32[]{:S(2)}, u32[]{:S(2)}) async-start(f32[128,96,2]{1,2,0:T(2,128)} %stack.2), calls=%async_computation.2 | async-start | bytes 262144 | tf_op jit(solution)/shard_map/all_to_all | solution.py:16
  32.9 11.8 %copy-start.9 = (f32[128]{0:T(128)S(1)}, f32[128]{0:T(128)}, u32[]{:S(2)}) copy-start(f32[128]{0:T(128)} %param.19) | copy-start | bytes 1540
  33.9 25.8 %all-to-all-start = ((f32[64,24,96]{2,1,0:T(8,128)}), f32[64,24,96]{2,1,0:T(8,128)S(1)}, u32[]{:S(2)}, u32[]{:S(2)}) async-start(f32[64,24,96]{2,1,0:T(8,128)} %broadcast_in_dim.57), calls=%async_computation | async-start | bytes 1572864 | tf_op jit(solution)/shard_map/all_to_all | solution.py:29
  66.5 1.2 copy-start.4
  66.5 1.2 copy-start.8
  86.3 6.3 %copy-start = (bf16[128,16384]{1,0:T(8,128)(2,1)S(1)}, bf16[128,16384]{1,0:T(8,128)(2,1)}, u32[]{:S(2)}) copy-start(bf16[128,16384]{1,0:T(8,128)(2,1)} %param.18) | copy-start | bytes 12582916
  93.8 5.7 %copy-start.6 = (f32[2]{0:T(128)S(1)}, f32[2]{0:T(128)}, u32[]{:S(2)}) copy-start(f32[2]{0:T(128)} %param.23) | copy-start | bytes 28
  93.8 6.3 %copy-start.10 = (s32[96]{0:T(128)S(1)}, s32[96]{0:T(128)}, u32[]{:S(2)}) copy-start(s32[96]{0:T(128)} %param.17) | copy-start | bytes 1156
  94.8 20.2 %all-to-all-start.5 = ((f32[64,24,128]{2,1,0:T(8,128)}), f32[64,24,128]{2,1,0:T(8,128)S(1)}, u32[]{:S(2)}, u32[]{:S(2)}) async-start(f32[64,24,128]{2,1,0:T(8,128)} %broadcast_in_dim.61), calls=%async_computation.5 | async-start | bytes 1572864 | tf_op jit(solution)/shard_map/all_to_all | solution.py:29
  121.4 8.7 %copy-start.7 = (bf16[96,24,256]{2,1,0:T(8,128)(2,1)S(1)}, bf16[96,24,256]{2,1,0:T(8,128)(2,1)}, u32[]{:S(2)}) copy-start(bf16[96,24,256]{2,1,0:T(8,128)(2,1)} %param.14) | copy-start | bytes 3538948
  189.4 6.3 %copy-start.1 = (bf16[128,16384]{1,0:T(8,128)(2,1)S(1)}, bf16[128,16384]{1,0:T(8,128)(2,1)}, u32[]{:S(2)}) copy-start(bf16[128,16384]{1,0:T(8,128)(2,1)} %param.18) | copy-start | bytes 12582916
